TPU v7x, 32 devices: a whole 2x2x4 slice. The times are simulated.
32 devices in a mesh: bank: 4 (over z), zero: 8 (over y, x, core).
Axes of the slice: x: 2, y: 2, z: 4, core: 2. Of those that a mesh axis runs over, the one named last changes fastest.
Arguments:
- master_gate: float32 [64, 2048, 1024], P('bank', 'zero'), may hold values from -0.1875 to 0.1875
- second_gate: bfloat16 [64, 2048, 1024], P('bank', 'zero'), may hold values from -0.0625 to 0.0625
- master_up: float32 [64, 2048, 1024], P('bank', 'zero'), may hold values from -0.1875 to 0.1875
- second_up: bfloat16 [64, 2048, 1024], P('bank', 'zero'), may hold values from -0.0625 to 0.0625
- master_down: float32 [64, 1024, 2048], P('bank', None, 'zero'), may hold values from -0.25 to 0.25
- second_down: bfloat16 [64, 1024, 2048], P('bank', None, 'zero'), may hold values from -0.09375 to 0.09375
- router_weight: float32 [2048, 64], P('zero', 'bank'), may hold values from -0.125 to 0.125
- router_gain: float32 [2048], P('zero'), may hold values from 0.25 to 1.75
Outputs:
- final_gate: bfloat16 [64, 2048, 1024], P('bank', None, 'zero')
- final_up: bfloat16 [64, 2048, 1024], P('bank', None, 'zero')
- final_down: bfloat16 [64, 1024, 2048], P('bank', 'zero')
- scale_gate: float32 [64, 1024], P('bank', 'zero')
- scale_up: float32 [64, 1024], P('bank', 'zero')
- scale_down: float32 [64, 1024], P('bank', 'zero')
- serve_router: bfloat16 [2048, 64], replicated
All inputs are finite; a program needn't handle non-finite values. Where the computation divides by a largest or mean magnitude, that divisor is 1e-20 or more.
Results may differ from a plain program's by a relative error of at most 0.001.
Values may be sent and summed in bfloat16 or wider, within the bound.
No kernel may reach another device: no remote copies, remote signals or barrier semaphores. Data moves between devices by JAX's collectives and lax.ppermute only.
A program may use at most 192 MiB of HBM per device.

v0:
```python
import jax
import jax.numpy as jnp
from jax import lax
from jax.sharding import PartitionSpec as P

D_MODEL = 2048


def on_device(
    master_gate,
    second_gate,
    master_up,
    second_up,
    master_down,
    second_down,
    router_weight,
    router_gain,
):
    merged_gate = master_gate + second_gate.astype(jnp.float32)
    merged_up = master_up + second_up.astype(jnp.float32)
    merged_down = master_down + second_down.astype(jnp.float32)
    total_gate, total_up, total_down = lax.psum(
        (
            jnp.sum(jnp.abs(merged_gate), axis=1),
            jnp.sum(jnp.abs(merged_up), axis=1),
            jnp.sum(jnp.abs(merged_down), axis=2),
        ),
        "zero",
    )
    scale_gate = total_gate / D_MODEL
    scale_up = total_up / D_MODEL
    scale_down = total_down / D_MODEL
    narrow_gate, narrow_up, narrow_down = (
        (merged_gate / jnp.expand_dims(scale_gate, 1)).astype(jnp.bfloat16),
        (merged_up / jnp.expand_dims(scale_up, 1)).astype(jnp.bfloat16),
        (merged_down / jnp.expand_dims(scale_down, 2)).astype(jnp.bfloat16),
    )
    final_gate, final_up = (
        lax.all_to_all(narrow_gate, "zero", split_axis=2, concat_axis=1, tiled=True),
        lax.all_to_all(narrow_up, "zero", split_axis=2, concat_axis=1, tiled=True),
    )
    final_down = lax.all_to_all(narrow_down, "zero", split_axis=1, concat_axis=2, tiled=True)
    scale_gate = lax.dynamic_slice_in_dim(
        scale_gate, lax.axis_index("zero") * final_gate.shape[2], final_gate.shape[2], axis=1
    )
    scale_up = lax.dynamic_slice_in_dim(
        scale_up, lax.axis_index("zero") * final_up.shape[2], final_up.shape[2], axis=1
    )
    scale_down = lax.dynamic_slice_in_dim(
        scale_down, lax.axis_index("zero") * final_down.shape[1], final_down.shape[1], axis=1
    )
    part_router = (router_weight * router_gain[:, None]).astype(jnp.bfloat16)
    row_router = lax.all_gather(part_router, "zero", axis=0, tiled=True)
    serve_router = lax.all_gather(row_router, "bank", axis=1, tiled=True)
    return (final_gate, final_up, final_down, scale_gate, scale_up, scale_down, serve_router)


def solution(mesh):
    return jax.shard_map(
        on_device,
        mesh=mesh,
        in_specs=(
            P("bank", "zero", None),
            P("bank", "zero", None),
            P("bank", "zero", None),
            P("bank", "zero", None),
            P("bank", None, "zero"),
            P("bank", None, "zero"),
            P("zero", "bank"),
            P("zero"),
        ),
        out_specs=(
            P("bank", None, "zero"),
            P("bank", None, "zero"),
            P("bank", "zero", None),
            P("bank", "zero"),
            P("bank", "zero"),
            P("bank", "zero"),
            P(),
        ),
        check_vma=False,
    )
```

profile of v0, /device:TPU:0, one launch (start us, length us, event | category | flops | bytes accessed | tf_op | source)
XLA Modules:
  0.0 554.7 jit_solution(10408405090956699153)
XLA Ops:
  7.2 0.0 all-reduce.3.cloned.1.call-start
  7.2 17.6 %copy.31 = f32[16,256,1024]{1,0,2:T(8,128)} copy(f32[16,256,1024]{2,1,0:T(8,128)} %param.8) | data formatting | bytes 33554432 | tf_op args[0]
  24.8 17.6 %copy.34 = f32[16,256,1024]{1,0,2:T(8,128)} copy(f32[16,256,1024]{2,1,0:T(8,128)} %param.10) | data formatting | bytes 33554432 | tf_op args[2]
  42.4 12.5 %copy.30 = bf16[16,256,1024]{1,0,2:T(8,128)(2,1)} copy(bf16[16,256,1024]{2,1,0:T(8,128)(2,1)} %param.9) | data formatting | bytes 16777216 | tf_op args[1]
  54.9 12.5 %copy.33 = bf16[16,256,1024]{1,0,2:T(8,128)(2,1)} copy(bf16[16,256,1024]{2,1,0:T(8,128)(2,1)} %param.11) | data formatting | bytes 16777216 | tf_op args[3]
  67.4 25.3 %abs_reduce_fusion = f32[16,1024]{0,1:T(8,128)} fusion(f32[16,1024,256]{2,1,0:T(8,128)} %param.12, bf16[16,1024,256]{2,1,0:T(8,128)(2,1)} %param.13), kind=kLoop, calls=%fused_computation.2 | loop fusion | flops 16760832 | bytes 25231360 | tf_op jit(solution)/shard_map/reduce_sum | solution.py:26
  92.7 0.0 copy-done
  92.7 0.0 copy-done.1
  92.7 13.2 %abs_reduce_fusion.1 = (f32[16,1024]{0,1:T(8,128)}, f32[16,1024]{0,1:T(8,128)}) fusion(f32[16,256,1024]{1,0,2:T(8,128)} %copy.34, bf16[16,256,1024]{1,0,2:T(8,128)(2,1)S(1)} %copy-done.1, f32[16,256,1024]{1,0,2:T(8,128)} %copy.31, bf16[16,256,1024]{1,0,2:T(8,128)(2,1)S(1)} %copy-done), kind=kLoop, calls=%fused_computation.4 | loop fusion | flops 33521664 | bytes 50462720 | tf_op jit(solution)/shard_map/reduce_sum | solution.py:25
  105.9 0.0 all-reduce.3.cloned.1.call-update
  105.9 62.0 %all-reduce.3.cloned.1.call-done = (f32[16,1024]{0,1:T(8,128)}, f32[16,1024]{0,1:T(8,128)}, f32[16,1024]{0,1:T(8,128)}) async-done(((f32[16,1024]{0,1:T(8,128)}, f32[16,1024]{0,1:T(8,128)}, f32[16,1024]{0,1:T(8,128)}), (f32[16,1024]{0,1:T(8,128)}, f32[16,1024]{0,1:T(8,128)}, f32[16,1024]{0,1:T(8,128)})) %all-reduce.3.cloned.1.call-update) | async-done | bytes 196624 | tf_op jit(solution)/shard_map/psum | solution.py:22
  167.9 1.1 broadcast_multiply_fusion.1
  169.0 12.0 %divide_convert_fusion.1 = bf16[16,256,1024]{1,0,2:T(8,128)(2,1)} fusion(f32[16,256,1024]{1,0,2:T(8,128)} %copy.34, bf16[16,256,1024]{1,0,2:T(8,128)(2,1)} %copy.33, f32[16,1024]{0,1:T(8,128)S(1)} %broadcast_multiply_fusion.1), kind=kLoop, calls=%fused_computation.3 | loop fusion | flops 16777216 | bytes 33619968 | tf_op jit(solution)/shard_map/convert_element_type | solution.py:35
  180.9 5.1 all-to-all-start.1
  186.0 0.0 copy-done.3
  186.1 12.0 %divide_convert_fusion.2 = bf16[16,256,1024]{1,0,2:T(8,128)(2,1)} fusion(f32[16,256,1024]{1,0,2:T(8,128)} %copy.31, bf16[16,256,1024]{1,0,2:T(8,128)(2,1)} %copy.30, f32[16,1024]{0,1:T(8,128)S(1)} %broadcast_multiply_fusion.2), kind=kLoop, calls=%fused_computation.6 | loop fusion | flops 16777216 | bytes 33619968 | tf_op jit(solution)/shard_map/convert_element_type | solution.py:34
  198.1 82.0 %all-to-all-done.1 = bf16[16,256,1024]{1,0,2:T(8,128)(2,1)} async-done(((bf16[16,256,1024]{1,0,2:T(8,128)(2,1)}), bf16[16,256,1024]{1,0,2:T(8,128)(2,1)}, u32[]{:S(2)}, u32[]{:S(2)}) %all-to-all-start.1) | async-done | bytes 8388640 | tf_op jit(solution)/shard_map/all_to_all | solution.py:40
  280.1 5.1 all-to-all-start
  285.3 23.8 %divide_convert_fusion = bf16[16,1024,256]{2,0,1:T(8,128)(2,1)} fusion(f32[16,1024,256]{2,1,0:T(8,128)} %param.12, f32[16,1024]{0,1:T(8,128)S(1)} %broadcast_multiply_fusion, bf16[16,1024,256]{2,1,0:T(8,128)(2,1)} %param.13), kind=kLoop, calls=%fused_computation.1 | loop fusion | flops 16777216 | bytes 33619968 | tf_op jit(solution)/shard_map/convert_element_type | solution.py:36
  309.0 70.0 %all-to-all-done = bf16[16,256,1024]{1,0,2:T(8,128)(2,1)} async-done(((bf16[16,256,1024]{1,0,2:T(8,128)(2,1)}), bf16[16,256,1024]{1,0,2:T(8,128)(2,1)}, u32[]{:S(2)}, u32[]{:S(2)}) %all-to-all-start) | async-done | bytes 8388640 | tf_op jit(solution)/shard_map/all_to_all | solution.py:39
  379.1 5.0 all-to-all-start.2
  384.1 97.2 %all_gather.6 = bf16[2048,16]{0,1:T(8,128)(2,1)S(1)} all-gather(bf16[256,16]{0,1:T(8,128)(2,1)S(1)} %multiply_convert_fusion), channel_id=1, replica_groups=mesh['bank'=4,'zero'=8] {'zero'}, dimensions={0}, use_global_device_ids=true | all-gather | bytes 73728 | tf_op jit(solution)/shard_map/all_gather | solution.py:53
  481.3 14.4 %all_gather.7 = bf16[2048,64]{0,1:T(8,128)(2,1)S(1)} all-gather(bf16[2048,16]{0,1:T(8,128)(2,1)S(1)} %all_gather.6), channel_id=1, replica_groups=mesh['bank'=4,'zero'=8] {'bank'}, dimensions={1}, use_global_device_ids=true | all-gather | bytes 327680 | tf_op jit(solution)/shard_map/all_gather | solution.py:54
  495.7 0.7 copy.39
  496.4 0.7 copy.40
  497.1 0.7 copy.41
  497.8 12.3 %copy.35 = bf16[16,8,256,128]{3,2,1,0:T(8,128)(2,1)} copy(bf16[16,8,256,128]{2,0,3,1:T(8,128)(2,1)} %bitcast.4) | data formatting | bytes 16777216 | tf_op jit(solution)/shard_map/all_to_all | solution.py:40
  510.0 12.3 %copy.32 = bf16[16,8,256,128]{3,2,1,0:T(8,128)(2,1)} copy(bf16[16,8,256,128]{2,0,3,1:T(8,128)(2,1)} %bitcast.1) | data formatting | bytes 16777216 | tf_op jit(solution)/shard_map/all_to_all | solution.py:39
  522.3 0.0 all-to-all-done.2
  522.3 11.4 %copy.38 = bf16[16,128,8,256]{3,2,1,0:T(8,128)(2,1)} copy(bf16[16,128,8,256]{3,0,1,2:T(8,128)(2,1)} %bitcast.7) | data formatting | bytes 16777216 | tf_op jit(solution)/shard_map/all_to_all | solution.py:42
  533.7 13.4 %all_to_all.50 = bf16[16,128,2048]{2,1,0:T(8,128)(2,1)} reshape(bf16[16,128,8,256]{3,2,1,0:T(8,128)(2,1)} %copy.38) | data formatting | bytes 16777216 | tf_op jit(solution)/shard_map/all_to_all | solution.py:42
  547.1 0.7 copy.53
  (15 shorter events, 0.1 us)
Async XLA Ops:
  7.2 160.7 %all-reduce.3.cloned.1.call-start = ((), (), s32[]{:S(2)}) async-start(), calls=%async_computation.3 | async-start | bytes 3145728 | tf_op jit(solution)/shard_map/psum | solution.py:22
  67.4 25.3 %copy-start = (bf16[16,256,1024]{1,0,2:T(8,128)(2,1)S(1)}, bf16[16,256,1024]{1,0,2:T(8,128)(2,1)}, u32[]{:S(2)}) copy-start(bf16[16,256,1024]{1,0,2:T(8,128)(2,1)} %copy.30) | copy-start | bytes 25165828
  67.4 25.3 %copy-start.1 = (bf16[16,256,1024]{1,0,2:T(8,128)(2,1)S(1)}, bf16[16,256,1024]{1,0,2:T(8,128)(2,1)}, u32[]{:S(2)}) copy-start(bf16[16,256,1024]{1,0,2:T(8,128)(2,1)} %copy.33) | copy-start | bytes 25165828
  180.9 5.1 copy-start.3
  180.9 99.1 %all-to-all-start.1 = ((bf16[16,256,1024]{1,0,2:T(8,128)(2,1)}), bf16[16,256,1024]{1,0,2:T(8,128)(2,1)}, u32[]{:S(2)}, u32[]{:S(2)}) async-start(bf16[16,256,1024]{1,0,2:T(8,128)(2,1)} %divide_convert_fusion.1), calls=%async_computation.1 | async-start | bytes 16777216 | tf_op jit(solution)/shard_map/all_to_all | solution.py:40
  198.1 87.1 %copy-start.2 = (f32[16,1024]{0,1:T(8,128)S(1)}, f32[16,1024]{0,1:T(8,128)}, u32[]{:S(2)}) copy-start(f32[16,1024]{0,1:T(8,128)} %get-tuple-element.16) | copy-start | bytes 196612
  280.1 99.0 %all-to-all-start = ((bf16[16,256,1024]{1,0,2:T(8,128)(2,1)}), bf16[16,256,1024]{1,0,2:T(8,128)(2,1)}, u32[]{:S(2)}, u32[]{:S(2)}) async-start(bf16[16,256,1024]{1,0,2:T(8,128)(2,1)} %divide_convert_fusion.2), calls=%async_computation | async-start | bytes 16777216 | tf_op jit(solution)/shard_map/all_to_all | solution.py:39
  309.0 75.1 %copy-start.4 = (f32[256,16]{0,1:T(8,128)S(1)}, f32[256,16]{0,1:T(8,128)}, u32[]{:S(2)}) copy-start(f32[256,16]{0,1:T(8,128)} %param.14) | copy-start | bytes 49156
  309.0 75.1 %copy-start.5 = (f32[256]{0:T(256)S(1)}, f32[256]{0:T(256)}, u32[]{:S(2)}) copy-start(f32[256]{0:T(256)} %param.15) | copy-start | bytes 3076
  379.1 143.3 %all-to-all-start.2 = ((bf16[16,1024,256]{2,0,1:T(8,128)(2,1)}), bf16[16,1024,256]{2,0,1:T(8,128)(2,1)}, u32[]{:S(2)}, u32[]{:S(2)}) async-start(bf16[16,1024,256]{2,0,1:T(8,128)(2,1)} %divide_convert_fusion), calls=%async_computation.2 | async-start | bytes 16777216 | tf_op jit(solution)/shard_map/all_to_all | solution.py:42
Sparse Core Ops, SparseCore 0:
  106.0 61.7 all-reduce.2
where the time goes:
time: 557 us; the launch traced here: 555 us
  waiting for transfers between devices  214 us (38%)
  local copies, waits for them, and re-layouts  112 us (20%)
  blocking collectives  112 us (20%)
  other arithmetic  87.4 us (16%)
  starting transfers between devices  15.3 us (3%)
  between operations  14.1 us (3%)
    all_gather x1, blocking collectives, on_device(): row_router = lax.all_gather(part_router, 'zero', axis=0, tiled=True)  97.2 us
    all_to_all x1, waiting for transfers between devices, on_device(): lax.all_to_all(narrow_up, 'zero', split_axis=2, concat_axis=1, tiled=True)  82 us
    all_to_all x1, waiting for transfers between devices, on_device(): lax.all_to_all(narrow_gate, 'zero', split_axis=2, concat_axis=1, tiled=True)  70 us
    unnamed x20, local copies, waits for them, and re-layouts  62.9 us
    psum x1, waiting for transfers between devices, on_device(): lax.psum((jnp.sum(jnp.abs(merged_gate), axis=1), jnp.sum(jnp.abs(merged_u...  62 us
    reduce_sum x1, other arithmetic, on_device(): jnp.sum(jnp.abs(merged_down), axis=2)  25.3 us
    all_to_all x2, local copies, waits for them, and re-layouts, on_device(): lax.all_to_all(narrow_down, 'zero', split_axis=1, concat_axis=2, tiled=True)  24.8 us
    convert_element_type x1, other arithmetic, on_device(): (merged_down / jnp.expand_dims(scale_down, 2)).astype(jnp.bfloat16)  23.8 us
  transfers between devices with their start and end apart: 4, of which 3 were waited for; matrix products, arithmetic and copies ran while one was open for 11% of the time, Pallas kernels for 0%

commit v1 on v0

--- a/solution.py
+++ b/solution.py
@@ -36,7 +36,12 @@
         (merged_down / jnp.expand_dims(scale_down, 2)).astype(jnp.bfloat16),
     )
     final_gate, final_up = (
-        lax.all_to_all(narrow_gate, "zero", split_axis=2, concat_axis=1, tiled=True),
+        jnp.concatenate(
+            lax.all_to_all(
+                jnp.stack(jnp.split(narrow_gate, lax.axis_size("zero"), axis=2)), "zero", 0, 0
+            ),
+            axis=1,
+        ),
         lax.all_to_all(narrow_up, "zero", split_axis=2, concat_axis=1, tiled=True),
     )
     final_down = lax.all_to_all(narrow_down, "zero", split_axis=1, concat_axis=2, tiled=True)

time: 557 us -> 522 us (0.937)
  local copies, waits for them, and re-layouts: 112 us -> 88.9 us
  waiting for transfers between devices: 214 us -> 202 us
    all_to_all x1, waiting for transfers between devices: 0.01 us -> 74.6 us  [on_device(): lax.all_to_all(narrow_down, 'zero', split_axis=1, concat_axis=2, tiled=True)]
    all_to_all x1, waiting for transfers between devices: 70 us -> 0.01 us  [on_device(): lax.all_to_all(jnp.stack(jnp.split(narrow_gate, lax.axis_size('zero'), ax...]
    unnamed x20 -> x18, local copies, waits for them, and re-layouts: 62.9 us -> 39.5 us
    all_to_all x1 -> x0, local copies, waits for them, and re-layouts: 12.3 us -> none  [on_device(): lax.all_to_all(narrow_gate, 'zero', split_axis=2, concat_axis=1, tiled=True)]
    all_to_all x1, waiting for transfers between devices: 82 us -> 69.8 us  [on_device(): lax.all_to_all(narrow_up, 'zero', split_axis=2, concat_axis=1, tiled=True)]
    reduce_sum x0 -> x1, other arithmetic: none -> 9.81 us  [on_device(): jnp.sum(jnp.abs(merged_gate), axis=1)]
    reshape x0 -> x1, local copies, waits for them, and re-layouts: none -> 7.89 us  [on_device(): jnp.concatenate(lax.all_to_all(jnp.stack(jnp.split(narrow_gate, lax.axis_...]
  transfers between devices with their start and end apart: 4 -> 4, of which waited for: 3 -> 3; matrix products, arithmetic and copies ran while one was open for 11% -> 13% of each run, Pallas kernels for 0% -> 0%
where the time goes in v1:
time: 522 us; the launch traced here: 521 us
  waiting for transfers between devices  202 us (39%)
  blocking collectives  111 us (21%)
  other arithmetic  89.4 us (17%)
  local copies, waits for them, and re-layouts  88.9 us (17%)
  starting transfers between devices  15.2 us (3%)
  between operations  14.2 us (3%)
    all_gather x1, blocking collectives, on_device(): row_router = lax.all_gather(part_router, 'zero', axis=0, tiled=True)  97.2 us
    all_to_all x1, waiting for transfers between devices, on_device(): lax.all_to_all(narrow_down, 'zero', split_axis=1, concat_axis=2, tiled=True)  74.6 us
    all_to_all x1, waiting for transfers between devices, on_device(): lax.all_to_all(narrow_up, 'zero', split_axis=2, concat_axis=1, tiled=True)  69.8 us
    psum x1, waiting for transfers between devices, on_device(): lax.psum((jnp.sum(jnp.abs(merged_gate), axis=1), jnp.sum(jnp.abs(merged_u...  57.2 us
    unnamed x18, local copies, waits for them, and re-layouts  39.5 us
    all_to_all x2, local copies, waits for them, and re-layouts, on_device(): lax.all_to_all(narrow_down, 'zero', split_axis=1, concat_axis=2, tiled=True)  24.8 us
    reduce_sum x1, other arithmetic, on_device(): jnp.sum(jnp.abs(merged_down), axis=2)  24.4 us
    convert_element_type x1, other arithmetic, on_device(): (merged_down / jnp.expand_dims(scale_down, 2)).astype(jnp.bfloat16)  23.8 us
  transfers between devices with their start and end apart: 4, of which 3 were waited for; matrix products, arithmetic and copies ran while one was open for 13% of the time, Pallas kernels for 0%

profile of v1, /device:TPU:0, one launch (start us, length us, event | category | flops | bytes accessed | tf_op | source)
XLA Modules:
  0.0 520.8 jit_solution(9076550071227375813)
XLA Ops:
  7.2 24.4 %abs_reduce_fusion = f32[16,1024]{0,1:T(8,128)S(1)} fusion(f32[16,1024,256]{2,1,0:T(8,128)} %param.12, bf16[16,1024,256]{2,1,0:T(8,128)(2,1)} %param.13), kind=kLoop, calls=%fused_computation.2 | loop fusion | flops 16760832 | bytes 25231360 | tf_op jit(solution)/shard_map/reduce_sum | solution.py:26
  31.6 0.8 copy.46
  32.4 12.5 %copy.39 = bf16[16,256,1024]{1,0,2:T(8,128)(2,1)} copy(bf16[16,256,1024]{2,1,0:T(8,128)(2,1)} %param.11) | data formatting | bytes 16777216 | tf_op args[3]
  44.9 17.6 %copy.40 = f32[16,256,1024]{1,0,2:T(8,128)} copy(f32[16,256,1024]{2,1,0:T(8,128)} %param.10) | data formatting | bytes 33554432 | tf_op args[2]
  62.5 9.1 %abs_reduce_fusion.1 = f32[16,1024]{0,1:T(8,128)S(1)} fusion(f32[16,256,1024]{1,0,2:T(8,128)} %copy.40, bf16[16,256,1024]{1,0,2:T(8,128)(2,1)} %copy.39), kind=kLoop, calls=%fused_computation.4 | loop fusion | flops 16760832 | bytes 25231360 | tf_op jit(solution)/shard_map/reduce_sum | solution.py:25
  71.6 0.8 copy.41
  72.4 9.8 %abs_reduce_fusion.2 = f32[16,1024]{1,0:T(8,128)} fusion(f32[16,256,1024]{2,1,0:T(8,128)} %param.8, bf16[16,256,1024]{2,1,0:T(8,128)(2,1)} %param.9), kind=kLoop, calls=%fused_computation.7 | loop fusion | flops 16760832 | bytes 25231360 | tf_op jit(solution)/shard_map/reduce_sum | solution.py:24
  82.3 57.2 %all-reduce.3.cloned.1.call-done = (f32[16,1024]{1,0:T(8,128)}, f32[16,1024]{1,0:T(8,128)}, f32[16,1024]{1,0:T(8,128)}) async-done(((f32[16,1024]{1,0:T(8,128)}, f32[16,1024]{1,0:T(8,128)}, f32[16,1024]{1,0:T(8,128)}), (f32[16,1024]{1,0:T(8,128)}, f32[16,1024]{1,0:T(8,128)}, f32[16,1024]{1,0:T(8,128)})) %all-reduce.3.cloned.1.call-update) | async-done | bytes 196624 | tf_op jit(solution)/shard_map/psum | solution.py:22
  139.5 0.8 broadcast_multiply_fusion.1
  140.6 12.0 %divide_convert_fusion.1 = bf16[16,256,1024]{1,0,2:T(8,128)(2,1)} fusion(f32[16,256,1024]{1,0,2:T(8,128)} %copy.40, bf16[16,256,1024]{1,0,2:T(8,128)(2,1)} %copy.39, f32[16,1024]{0,1:T(8,128)S(1)} %copy.42), kind=kLoop, calls=%fused_computation.3 | loop fusion | flops 16777216 | bytes 33619968 | tf_op jit(solution)/shard_map/convert_element_type | solution.py:35
  152.5 5.3 %all-to-all-start.1 = ((bf16[16,256,1024]{1,0,2:T(8,128)(2,1)}), bf16[16,256,1024]{1,0,2:T(8,128)(2,1)}, u32[]{:S(2)}, u32[]{:S(2)}) async-start(bf16[16,256,1024]{1,0,2:T(8,128)(2,1)} %divide_convert_fusion.1), calls=%async_computation.1 | async-start | bytes 16777216 | tf_op jit(solution)/shard_map/all_to_all | solution.py:45
  158.1 23.8 %divide_convert_fusion = bf16[16,1024,256]{2,0,1:T(8,128)(2,1)} fusion(f32[16,1024,256]{2,1,0:T(8,128)} %param.12, f32[16,1024]{0,1:T(8,128)S(1)} %copy.47, bf16[16,1024,256]{2,1,0:T(8,128)(2,1)} %param.13), kind=kLoop, calls=%fused_computation.1 | loop fusion | flops 16777216 | bytes 33619968 | tf_op jit(solution)/shard_map/convert_element_type | solution.py:36
  181.9 69.8 %all-to-all-done.1 = bf16[16,256,1024]{1,0,2:T(8,128)(2,1)} async-done(((bf16[16,256,1024]{1,0,2:T(8,128)(2,1)}), bf16[16,256,1024]{1,0,2:T(8,128)(2,1)}, u32[]{:S(2)}, u32[]{:S(2)}) %all-to-all-start.1) | async-done | bytes 8388640 | tf_op jit(solution)/shard_map/all_to_all | solution.py:45
  251.7 4.9 all-to-all-start.2
  256.7 9.4 %divide_convert_fusion.2 = bf16[16,256,1024]{2,1,0:T(8,128)(2,1)S(1)} fusion(f32[16,256,1024]{2,1,0:T(8,128)} %param.8, bf16[16,256,1024]{2,1,0:T(8,128)(2,1)} %param.9, f32[16,1024]{1,0:T(8,128)S(1)} %broadcast_multiply_fusion.2), kind=kLoop, calls=%fused_computation.6 | loop fusion | flops 16777216 | bytes 33619968 | tf_op jit(solution)/shard_map/convert_element_type | solution.py:34
  266.1 1.2 fusion.7
  267.4 1.2 fusion.6
  268.6 1.2 fusion.5
  269.9 1.2 fusion.4
  271.1 1.2 fusion.3
  272.3 1.2 fusion.2
  273.6 1.2 fusion.1
  274.8 1.2 fusion
  276.1 74.6 %all-to-all-done.2 = bf16[16,1024,256]{2,0,1:T(8,128)(2,1)} async-done(((bf16[16,1024,256]{2,0,1:T(8,128)(2,1)}), bf16[16,1024,256]{2,0,1:T(8,128)(2,1)}, u32[]{:S(2)}, u32[]{:S(2)}) %all-to-all-start.2) | async-done | bytes 8388640 | tf_op jit(solution)/shard_map/all_to_all | solution.py:47
  350.7 4.9 all-to-all-start
  355.7 97.2 %all_gather.6 = bf16[2048,16]{0,1:T(8,128)(2,1)S(1)} all-gather(bf16[256,16]{0,1:T(8,128)(2,1)S(1)} %multiply_convert_fusion), channel_id=1, replica_groups=mesh['bank'=4,'zero'=8] {'zero'}, dimensions={0}, use_global_device_ids=true | all-gather | bytes 73728 | tf_op jit(solution)/shard_map/all_gather | solution.py:58
  452.9 14.2 %all_gather.7 = bf16[2048,64]{0,1:T(8,128)(2,1)S(1)} all-gather(bf16[2048,16]{0,1:T(8,128)(2,1)S(1)} %all_gather.6), channel_id=1, replica_groups=mesh['bank'=4,'zero'=8] {'bank'}, dimensions={1}, use_global_device_ids=true | all-gather | bytes 327680 | tf_op jit(solution)/shard_map/all_gather | solution.py:59
  468.3 12.3 %copy.43 = bf16[16,8,256,128]{3,2,1,0:T(8,128)(2,1)} copy(bf16[16,8,256,128]{2,0,3,1:T(8,128)(2,1)} %bitcast.11) | data formatting | bytes 16777216 | tf_op jit(solution)/shard_map/all_to_all | solution.py:45
  480.6 11.4 %copy.48 = bf16[16,128,8,256]{3,2,1,0:T(8,128)(2,1)} copy(bf16[16,128,8,256]{3,0,1,2:T(8,128)(2,1)} %bitcast.14) | data formatting | bytes 16777216 | tf_op jit(solution)/shard_map/all_to_all | solution.py:47
  492.0 13.4 %all_to_all.37 = bf16[16,128,2048]{2,1,0:T(8,128)(2,1)} reshape(bf16[16,128,8,256]{3,2,1,0:T(8,128)(2,1)} %copy.48) | data formatting | bytes 16777216 | tf_op jit(solution)/shard_map/all_to_all | solution.py:47
  505.4 7.9 %copy.38 = bf16[16,8,256,128]{3,2,1,0:T(8,128)(2,1)} copy(bf16[16,8,256,128]{3,2,0,1:T(8,128)(2,1)} %bitcast.8) | data formatting | bytes 16777216 | tf_op jit(solution)/shard_map/reshape | solution.py:39
  513.3 0.7 copy.67
  (18 shorter events, 1.7 us)
Async XLA Ops:
  7.2 132.3 %all-reduce.3.cloned.1.call-start = ((), (), s32[]{:S(2)}) async-start(), calls=%async_computation.3 | async-start | bytes 393216 | tf_op jit(solution)/shard_map/psum | solution.py:22
  152.5 5.3 %copy-start.1 = (f32[16,1024]{1,0:T(8,128)S(1)}, f32[16,1024]{1,0:T(8,128)}, u32[]{:S(2)}) copy-start(f32[16,1024]{1,0:T(8,128)} %get-tuple-element.16) | copy-start | bytes 196612
  152.5 99.2 %all-to-all-start.1 = ((bf16[16,256,1024]{1,0,2:T(8,128)(2,1)}), bf16[16,256,1024]{1,0,2:T(8,128)(2,1)}, u32[]{:S(2)}, u32[]{:S(2)}) async-start(bf16[16,256,1024]{1,0,2:T(8,128)(2,1)} %divide_convert_fusion.1), calls=%async_computation.1 | async-start | bytes 16777216 | tf_op jit(solution)/shard_map/all_to_all | solution.py:45
  181.9 74.8 %copy-start = (f32[16,1024]{1,0:T(8,128)S(1)}, f32[16,1024]{1,0:T(8,128)}, u32[]{:S(2)}) copy-start(f32[16,1024]{1,0:T(8,128)} %get-tuple-element.14) | copy-start | bytes 196612
  251.7 99.0 %all-to-all-start.2 = ((bf16[16,1024,256]{2,0,1:T(8,128)(2,1)}), bf16[16,1024,256]{2,0,1:T(8,128)(2,1)}, u32[]{:S(2)}, u32[]{:S(2)}) async-start(bf16[16,1024,256]{2,0,1:T(8,128)(2,1)} %divide_convert_fusion), calls=%async_computation.2 | async-start | bytes 16777216 | tf_op jit(solution)/shard_map/all_to_all | solution.py:47
  276.1 79.6 %copy-start.2 = (f32[256,16]{0,1:T(8,128)S(1)}, f32[256,16]{0,1:T(8,128)}, u32[]{:S(2)}) copy-start(f32[256,16]{0,1:T(8,128)} %param.14) | copy-start | bytes 49156
  276.1 79.6 %copy-start.3 = (f32[256]{0:T(256)S(1)}, f32[256]{0:T(256)}, u32[]{:S(2)}) copy-start(f32[256]{0:T(256)} %param.15) | copy-start | bytes 3076
  350.7 154.7 %all-to-all-start = ((bf16[8,16,256,128]{3,2,1,0:T(8,128)(2,1)}), bf16[8,16,256,128]{3,2,1,0:T(8,128)(2,1)}, u32[]{:S(2)}, u32[]{:S(2)}) async-start(bf16[8,16,256,128]{3,2,1,0:T(8,128)(2,1)} %fusion), calls=%async_computation | async-start | bytes 16777216 | tf_op jit(solution)/shard_map/all_to_all | solution.py:40
Sparse Core Ops, SparseCore 0:
  82.4 57.0 all-reduce.2
